TPU v7x, 32 devices: a whole 2x2x4 slice. The times are simulated.
32 devices in a mesh: pts: 16 (over z, y, x), rows: 2 (over core).
Axes of the slice: x: 2, y: 2, z: 4, core: 2. Of those that a mesh axis runs over, the one named last changes fastest.
Arguments:
- vertex: bfloat16 [16, 960, 960], P('pts', 'rows'), may hold values from -0.1875 to 0.1875
- bubble: float32 [16, 960], P('pts'), may hold values from -2 to -0.2
- cross_deriv: bfloat16 [16, 960, 960], P('pts', 'rows'), may hold values from -6 to 6
- send_blocks: int32 [16, 16, 2], P('pts'), may hold values from -1 to 14, as said below
- recv_slots: int32 [16, 15], P('pts'), may hold values from 0 to 31, as said below
- freq_shift: int32 [16, 15], P('pts'), may hold values from -16 to 16
- proj_coef: float32 [16, 15], P('pts'), may hold values from -1.5 to 1.5
Outputs:
- left_insertion: bfloat16 [16, 960, 960], P('pts', 'rows')
Inputs may be any that keep to these rules, and one draw needn't show every extreme that they name: `send_blocks`: entry [d, e, c] is -1 for an empty slot, else the index p * 15 + g of the box (local point p, form factor g) of device d along pts that fills slot c towards device e. For every e some d fills all 2 slots towards e. `recv_slots`: entry [q, f] is 2 * d + c for a slot c towards device q // 1 along pts whose send_blocks entry [d, q, c] is not -1; each such slot is named by exactly one entry of that device's points.
All inputs are finite; a program needn't handle non-finite values.
Results may differ from a plain program's by a relative error of at most 0.0058.
Values may be sent and summed in bfloat16 or wider, within the bound.
No kernel may reach another device: no remote copies, remote signals or barrier semaphores. Data moves between devices by JAX's collectives and lax.ppermute only.
A program may use at most 128 MiB of HBM per device.

v0:
```python
import jax
import jax.numpy as jnp
from jax import lax
from jax.sharding import PartitionSpec as P


def add_rows(left_cols, panel):
    return jnp.dot(left_cols, panel, preferred_element_type=jnp.float32)


def body(vertex, bubble, cross_deriv, send_blocks, recv_slots, freq_shift, proj_coef):
    points, rows_here, width_all = vertex.shape
    form_count = recv_slots.shape[1]
    matsubara_number = width_all // form_count
    local_boxes = cross_deriv.reshape(points, rows_here, form_count, matsubara_number).transpose(
        0, 2, 1, 3
    )
    local_boxes = local_boxes.reshape(points * form_count, rows_here, matsubara_number)
    wanted = send_blocks[0]
    outgoing = jnp.where(
        (wanted >= 0)[:, :, None, None],
        local_boxes[jnp.clip(wanted, 0, points * form_count - 1)],
        jnp.zeros((), jnp.bfloat16),
    )
    incoming = lax.all_to_all(outgoing, "pts", split_axis=0, concat_axis=0, tiled=True)
    arrived = incoming.reshape(-1, rows_here, matsubara_number)
    picked = arrived[recv_slots]
    source_grid = jnp.arange(matsubara_number, dtype=jnp.int32)
    target_freq = source_grid[None, None, None, :] + freq_shift[:, :, None, None]
    selector = (source_grid[None, None, :, None] == target_freq).astype(jnp.bfloat16)
    shifted = jnp.einsum("pfrm,pfmn->pfrn", picked, selector, preferred_element_type=jnp.float32)
    box_values = (shifted * proj_coef[:, :, None, None]).astype(jnp.bfloat16)
    remapped = box_values.transpose(0, 2, 1, 3).reshape(points, rows_here, width_all)
    scaled = (vertex.astype(jnp.float32) * bubble[:, None, :]).astype(jnp.bfloat16)
    outputs = [add_rows(scaled[0], lax.all_gather(remapped[0], "rows", axis=0, tiled=True))]
    result = jnp.stack(outputs)
    return result.astype(jnp.bfloat16)


def solution(mesh):
    in_specs = (
        P("pts", "rows", None),
        P("pts", None),
        P("pts", "rows", None),
        P("pts", None, None),
        P("pts", None),
        P("pts", None),
        P("pts", None),
    )
    out_specs = P("pts", "rows", None)
    return jax.shard_map(body, mesh=mesh, in_specs=in_specs, out_specs=out_specs, check_vma=False)
```

profile of v0, /device:TPU:0, one launch (start us, length us, event | category | flops | bytes accessed | tf_op | source)
XLA Modules:
  0.0 91.7 jit_solution(13739622224468688063)
XLA Ops:
  6.5 0.7 compare_select_fusion
  7.2 0.7 compare_bitcast_fusion
  7.9 1.7 %copy.14 = bf16[1,480,960]{1,2,0:T(8,128)(2,1)S(1)} copy(bf16[1,480,960]{2,1,0:T(8,128)(2,1)} %param.9) | data formatting | bytes 1843200 | tf_op args[2]
  9.6 0.1 copy.15
  9.7 0.1 reshape.86
  9.8 0.1 copy.13
  9.9 0.7 gather_fusion
  10.6 1.5 %broadcast_select_fusion = bf16[16,2,480,64]{2,3,1,0:T(8,128)(2,1)} fusion(bf16[16,2,480,64]{2,3,1,0:T(8,128)(2,1)S(1)} %bitcast.31, pred[16,2]{1,0:T(8,128)(4,1)S(1)} %copy.13), kind=kLoop, calls=%fused_computation.2 | loop fusion | flops 983040 | bytes 3932192 | tf_op jit(solution)/shard_map/jit(_where)/select_n | solution.py:20
  12.1 8.5 %all-to-all-start = ((bf16[16,2,480,64]{2,3,1,0:T(8,128)(2,1)}), bf16[16,2,480,64]{2,3,1,0:T(8,128)(2,1)S(1)}, u32[]{:S(2)}, u32[]{:S(2)}) async-start(bf16[16,2,480,64]{2,3,1,0:T(8,128)(2,1)} %broadcast_select_fusion), calls=%async_computation | async-start | bytes 4194304 | tf_op jit(solution)/shard_map/all_to_all | solution.py:25
  20.6 0.0 copy-start
  20.6 0.0 all-gather.2.cloned.1.call-start
  20.7 0.0 copy-done.4
  20.7 0.0 copy-done.1
  20.7 0.1 iota_add_fusion
  20.8 42.9 %all-to-all-done = bf16[16,2,480,64]{2,3,1,0:T(8,128)(2,1)S(1)} async-done(((bf16[16,2,480,64]{2,3,1,0:T(8,128)(2,1)}), bf16[16,2,480,64]{2,3,1,0:T(8,128)(2,1)S(1)}, u32[]{:S(2)}, u32[]{:S(2)}) %all-to-all-start) | async-done | bytes 1966112 | tf_op jit(solution)/shard_map/all_to_all | solution.py:25
  63.6 0.6 gather_fusion.1
  64.2 0.0 copy-done
  64.3 0.5 multiply_convert_fusion
  64.7 0.0 copy-start.2
  64.7 0.0 copy-start.3
  64.8 1.4 %copy.16 = bf16[480,960]{1,0:T(8,128)(2,1)} copy(bf16[480,960]{0,1:T(8,128)(2,1)S(1)} %bitcast.33) | data formatting | bytes 1843200 | tf_op jit(solution)/shard_map/squeeze;reshape | solution.py:35
  66.2 0.0 all-gather.2.cloned.1.call-update
  66.2 14.9 %all-gather.2.cloned.1.call-done = bf16[960,960]{1,0:T(8,128)(2,1)} async-done(((bf16[480,960]{1,0:T(8,128)(2,1)}), bf16[960,960]{1,0:T(8,128)(2,1)}) %all-gather.2.cloned.1.call-update) | async-done | bytes 1843216 | tf_op jit(solution)/shard_map/all_gather | solution.py:35
  81.1 3.7 %fusion = bf16[1,480,960]{2,1,0:T(8,128)(2,1)} fusion(bf16[960,960]{1,0:T(8,128)(2,1)} %all-gather.2.cloned.1.call-done, bf16[1,480,960]{2,1,0:T(8,128)(2,1)S(1)} %copy-done.2, f32[960]{0:T(1024)S(1)} %bitcast.36), kind=kOutput, calls=%fused_computation.6 | convolution fusion | flops 886579200 | bytes 3690240 | tf_op jit(solution)/shard_map/dot_general | solution.py:8
  (7 shorter events, 0.0 us)
Async XLA Ops:
  12.1 8.5 %copy-start.4 = (s32[1,15]{1,0:T(1,128)S(1)}, s32[1,15]{1,0:T(1,128)}, u32[]{:S(2)}) copy-start(s32[1,15]{1,0:T(1,128)} %param.11) | copy-start | bytes 184
  12.1 8.6 %copy-start.1 = (s32[1,15]{1,0:T(1,128)S(1)}, s32[1,15]{1,0:T(1,128)}, u32[]{:S(2)}) copy-start(s32[1,15]{1,0:T(1,128)} %param.12) | copy-start | bytes 184
  12.1 51.5 %all-to-all-start = ((bf16[16,2,480,64]{2,3,1,0:T(8,128)(2,1)}), bf16[16,2,480,64]{2,3,1,0:T(8,128)(2,1)S(1)}, u32[]{:S(2)}, u32[]{:S(2)}) async-start(bf16[16,2,480,64]{2,3,1,0:T(8,128)(2,1)} %broadcast_select_fusion), calls=%async_computation | async-start | bytes 4194304 | tf_op jit(solution)/shard_map/all_to_all | solution.py:25
  20.6 43.7 %copy-start = (f32[1,15]{1,0:T(1,128)S(1)}, f32[1,15]{1,0:T(1,128)}, u32[]{:S(2)}) copy-start(f32[1,15]{1,0:T(1,128)} %param.13) | copy-start | bytes 184
  20.6 60.5 %all-gather.2.cloned.1.call-start = ((), (), s32[]{:S(2)}) async-start(), calls=%async_computation.1 | async-start | bytes 2949120 | tf_op jit(solution)/shard_map/all_gather | solution.py:35
  64.7 16.4 %copy-start.2 = (bf16[1,480,960]{2,1,0:T(8,128)(2,1)S(1)}, bf16[1,480,960]{2,1,0:T(8,128)(2,1)}, u32[]{:S(2)}) copy-start(bf16[1,480,960]{2,1,0:T(8,128)(2,1)} %param.7) | copy-start | bytes 2764804
  64.7 16.4 %copy-start.3 = (f32[1,960]{1,0:T(1,128)S(1)}, f32[1,960]{1,0:T(1,128)}, u32[]{:S(2)}) copy-start(f32[1,960]{1,0:T(1,128)} %param.8) | copy-start | bytes 11524
Sparse Core Ops, SparseCore 0:
  66.3 14.7 all-gather.1
where the time goes:
time: 91.9 us; the launch traced here: 91.7 us
  waiting for transfers between devices  57.8 us (63%)
  between operations  13.5 us (15%)
  starting transfers between devices  8.51 us (9%)
  local copies, waits for them, and re-layouts  4.68 us (5%)
  matrix products  4.15 us (5%)
  other arithmetic  3 us (3%)
    all_to_all x1, waiting for transfers between devices, body(): lax.all_to_all(outgoing, 'pts', split_axis=0, concat_axis=0, tiled=True)  42.9 us
    all_gather x1, waiting for transfers between devices, body(): lax.all_gather(remapped[0], 'rows', axis=0, tiled=True)  14.9 us
    all_to_all x1, starting transfers between devices, body(): lax.all_to_all(outgoing, 'pts', split_axis=0, concat_axis=0, tiled=True)  8.47 us
    dot_general x1, matrix products, add_rows(): return jnp.dot(left_cols, panel, preferred_element_type=jnp.float32)  3.68 us
  transfers between devices with their start and end apart: 2, of which 2 were waited for; matrix products, arithmetic and copies ran while one was open for 0% of the time, Pallas kernels for 0%

commit v1 on v0

v1 whole, which is shorter than its diff:
```python
import functools

import jax
import jax.numpy as jnp
from jax import lax
from jax.experimental import pallas as pl
from jax.experimental.pallas import tpu as pltpu
from jax.sharding import PartitionSpec as P


LIMIT = 24 * 1024 * 1024


def partner_of(n, me, k):
    return me ^ k if n & (n - 1) == 0 else lax.rem(me + k, n)


def origin_of(n, me, k):
    return me ^ k if n & (n - 1) == 0 else lax.rem(me - k + n, n)


def pack_kernel(n, boxes, width, blocks_ref, cross_ref, *rest):
    slabs, table = rest[:n], rest[n]
    me = lax.axis_index("pts")
    rows = cross_ref.shape[1]
    low = lax.broadcasted_iota(jnp.int32, (rows, 2 * width), 1) < width
    for t in range(boxes // 2):
        tile = cross_ref[0, :, 2 * width * t : 2 * width * (t + 1)]
        turned = jnp.concatenate([tile[:, width:], tile[:, :width]], axis=1)
        table[2 * t] = jnp.where(low, tile, turned)
        table[2 * t + 1] = jnp.where(low, turned, tile)
    if boxes % 2:
        last = cross_ref[0, :, width * (boxes - 1) : width * boxes]
        table[boxes - 1] = jnp.concatenate([last, last], axis=1)
    for k in range(n):
        dest = partner_of(n, me, k)
        first = jnp.clip(blocks_ref[0, 0, dest], 0, boxes - 1)
        second = jnp.clip(blocks_ref[0, 1, dest], 0, boxes - 1)
        slabs[k][...] = jnp.where(low, table[first], table[second])


def consume_kernel(n, boxes, width, group, first, last, *refs):
    fills_ref, shift_ref, coef_ref, mine_ref, other_ref = refs[:5]
    slabs = refs[5 : 5 + 2 * len(group)]
    held = refs[5 + 2 * len(group) :]
    total = held[-1]
    me = lax.axis_index("pts")
    rows = mine_ref.shape[0]
    lane = lax.broadcasted_iota(jnp.int32, (rows, 2 * width), 1)
    if last and not first:
        for t in range((boxes + 1) // 2):
            total[t] = held[0][t]
    for i, k in enumerate(group):
        product = jnp.dot(mine_ref[...], slabs[2 * i][...], preferred_element_type=jnp.float32)
        product += jnp.dot(other_ref[...], slabs[2 * i + 1][...], preferred_element_type=jnp.float32)
        source = origin_of(n, me, k)
        for c in range(2):
            f = fills_ref[2 * source + c]

            @pl.when(f >= 0)
            def _():
                h, t = lax.rem(f, 2), f // 2
                shift = shift_ref[0, f]
                amount = lax.rem(width * h - width * c - shift + 4 * width, 2 * width)
                moved = pltpu.roll(product, amount, 1) * coef_ref[0, f]
                taken = lane - width * h + shift
                value = jnp.where((taken >= 0) & (taken < width), moved, 0.0)
                here = lane // width == h
                total[t] = jnp.where(here, value, total[t].astype(jnp.float32)).astype(total.dtype)

    if last:
        out_ref = held[-2]
        for t in range((boxes + 1) // 2):
            if 2 * t + 1 < boxes:
                out_ref[0, :, 2 * width * t : 2 * width * (t + 1)] = total[t]
            else:
                out_ref[0, :, 2 * width * t : width * boxes] = total[t][:, :width]


def plan(n):
    far = list(range(n - 1, n // 2 - 1, -1))
    near = list(range(1, n // 2))
    sequence = []
    for i, k in enumerate(far):
        sequence.append(k)
        if i >= 1 and i - 1 < len(near):
            sequence.append(near[i - 1])
    groups = [[0] + near[: len(near) // 2], near[len(near) // 2 :]]
    groups += [far[i : i + 2] for i in range(0, len(far) - 2, 2)] + [[far[-2]], [far[-1]]]
    return sequence, groups


def body(n, vertex, bubble, cross_deriv, send_blocks, recv_slots, freq_shift, proj_coef):
    _, rows, order = vertex.shape
    boxes = recv_slots.shape[1]
    width = order // boxes
    side = lax.axis_index("rows")
    power = n & (n - 1) == 0

    def pairs(k):
        return [(i, i ^ k if power else (i + k) % n) for i in range(n)]

    smem = pl.BlockSpec(memory_space=pltpu.SMEM)
    vmem = pl.BlockSpec(memory_space=pltpu.VMEM)
    slabs = pl.pallas_call(
        functools.partial(pack_kernel, n, boxes, width),
        out_shape=[jax.ShapeDtypeStruct((rows, 2 * width), cross_deriv.dtype)] * n,
        in_specs=[smem, vmem],
        out_specs=[vmem] * n,
        scratch_shapes=[pltpu.VMEM((boxes, rows, 2 * width), cross_deriv.dtype)],
        cost_estimate=pl.CostEstimate(flops=2000000, bytes_accessed=3000000, transcendentals=0),
        compiler_params=pltpu.CompilerParams(vmem_limit_bytes=LIMIT),
        name="pack",
    )(send_blocks.transpose(0, 2, 1), cross_deriv)

    scaled = (vertex[0].astype(jnp.float32) * bubble[0][None, :]).astype(jnp.bfloat16)
    mine = jnp.where(side == 0, scaled[:, :rows], scaled[:, rows:])
    other = jnp.where(side == 0, scaled[:, rows:], scaled[:, :rows])
    named = recv_slots[0][None, :] == jnp.arange(2 * n, dtype=jnp.int32)[:, None]
    fills = jnp.max(jnp.where(named, jnp.arange(boxes, dtype=jnp.int32)[None, :], -1), axis=1)

    sequence, groups = plan(n)
    arrived, across = {0: slabs[0]}, {}
    for k in sequence:
        arrived[k] = lax.ppermute(slabs[k], "pts", pairs(k))
    for k in sum(groups, []):
        across[k] = lax.ppermute(arrived[k], "rows", [(0, 1), (1, 0)])

    tiles = jax.ShapeDtypeStruct(((boxes + 1) // 2, rows, 2 * width), jnp.bfloat16)
    total = None
    for i, group in enumerate(groups):
        first, last = i == 0, i == len(groups) - 1
        operands = [fills, freq_shift, proj_coef, mine, other]
        for k in group:
            operands += [arrived[k], across[k]]
        specs = [smem] * 3 + [vmem] * (len(operands) - 3)
        if not first:
            operands.append(total)
            specs.append(vmem)
        total = pl.pallas_call(
            functools.partial(consume_kernel, n, boxes, width, group, first, last),
            out_shape=jax.ShapeDtypeStruct(vertex.shape, jnp.bfloat16) if last else tiles,
            in_specs=specs,
            out_specs=vmem,
            scratch_shapes=[pltpu.VMEM(tiles.shape, tiles.dtype)] if last else [],
            input_output_aliases={} if first or last else {len(operands) - 1: 0},
            cost_estimate=pl.CostEstimate(
                flops=2 * rows * order * 2 * width * len(group), bytes_accessed=3000000, transcendentals=0
            ),
            compiler_params=pltpu.CompilerParams(vmem_limit_bytes=LIMIT),
        )(*operands)
    return total


def solution(mesh):
    in_specs = (
        P("pts", "rows", None),
        P("pts", None),
        P("pts", "rows", None),
        P("pts", None, None),
        P("pts", None),
        P("pts", None),
        P("pts", None),
    )
    out_specs = P("pts", "rows", None)
    n = mesh.shape["pts"]

    def run(*args):
        return body(n, *args)

    return jax.shard_map(run, mesh=mesh, in_specs=in_specs, out_specs=out_specs, check_vma=False)
```

time: 91.9 us -> 86.1 us (0.937)
  waiting for transfers between devices: 57.8 us -> 16.5 us
  starting transfers between devices: 8.51 us -> 45.9 us
  Pallas kernels: 0 us -> 18.7 us
  between operations: 13.5 us -> 0.15 us
  matrix products: 4.15 us -> 0 us
  local copies, waits for them, and re-layouts: 4.68 us -> 1.9 us
    ppermute x0 -> x31, starting transfers between devices: none -> 45.9 us  [the longest x15 42.7 us: body(): arrived[k] = lax.ppermute(slabs[k], 'pts', pairs(k))]
    all_to_all x1 -> x0, waiting for transfers between devices: 42.9 us -> none  [body(): lax.all_to_all(outgoing, 'pts', split_axis=0, concat_axis=0, tiled=True)]
    pallas_call x0 -> x8, Pallas kernels: none -> 18.7 us  [the longest x7 17.2 us: body(): pl.pallas_call(functools.partial(consume_kernel, n, boxes, width, group,...]
    ppermute x0 -> x31, waiting for transfers between devices: none -> 16.5 us  [the longest x15 16.4 us: body(): arrived[k] = lax.ppermute(slabs[k], 'pts', pairs(k))]
    all_gather x1 -> x0, waiting for transfers between devices: 14.9 us -> none  [body(): lax.all_gather(remapped[0], 'rows', axis=0, tiled=True)]
    all_to_all x1 -> x0, starting transfers between devices: 8.47 us -> none  [body(): lax.all_to_all(outgoing, 'pts', split_axis=0, concat_axis=0, tiled=True)]
    dot_general x2 -> x0, matrix products: 4.15 us -> none  [the longest x1 3.68 us: add_rows(): return jnp.dot(left_cols, panel, preferred_element_type=jnp.float32)]
    another operation x1 -> x0, local copies, waits for them, and re-layouts: 1.43 us -> none  [body(): remapped[0]]
  transfers between devices with their start and end apart: 2 -> 31, of which waited for: 2 -> 6; matrix products, arithmetic and copies ran while one was open for 0% -> 3% of each run, Pallas kernels for 0% -> 17%
where the time goes in v1:
time: 86.1 us; the launch traced here: 85.9 us
  starting transfers between devices  45.9 us (53%)
  Pallas kernels  18.7 us (22%)
  waiting for transfers between devices  16.5 us (19%)
  other arithmetic  2.69 us (3%)
  local copies, waits for them, and re-layouts  1.9 us (2%)
    ppermute x15, starting transfers between devices, body(): arrived[k] = lax.ppermute(slabs[k], 'pts', pairs(k))  42.7 us
    pallas_call x7, Pallas kernels, body(): pl.pallas_call(functools.partial(consume_kernel, n, boxes, width, group,...  17.2 us
    ppermute x15, waiting for transfers between devices, body(): arrived[k] = lax.ppermute(slabs[k], 'pts', pairs(k))  16.4 us
    ppermute x16, starting transfers between devices, body(): across[k] = lax.ppermute(arrived[k], 'rows', [(0, 1), (1, 0)])  3.26 us
    unnamed x14, local copies, waits for them, and re-layouts  1.9 us
  transfers between devices with their start and end apart: 31, of which 6 were waited for; matrix products, arithmetic and copies ran while one was open for 3% of the time, Pallas kernels for 17%

profile of v1, /device:TPU:0, one launch (start us, length us, event | category | flops | bytes accessed | tf_op | source)
XLA Modules:
  0.0 85.9 jit_solution(6532484481186596341)
XLA Ops:
  1.9 1.5 %pack.1 = (bf16[480,128]{1,0:T(8,128)(2,1)S(1)}, bf16[480,128]{1,0:T(8,128)(2,1)S(1)}, bf16[480,128]{1,0:T(8,128)(2,1)S(1)}, bf16[480,128]{1,0:T(8,128)(2,1)S(1)...) custom-call(s32[1,2,16]{2,1,0:T(2,128)S(1)} %bitcast.6, ...), custom_call_target="tpu_custom_call" | custom-call | flops 2000000 | bytes 3000000 | tf_op jit(solution)/shard_map/pack/pallas_call | solution.py:105
  3.4 3.0 %collective-permute-start.25 = (bf16[480,128]{1,0:T(8,128)(2,1)S(1)}, bf16[480,128]{1,0:T(8,128)(2,1)S(1)}, u32[]{:S(2)}, u32[]{:S(2)}) collective-permute-start(bf16[480,128]{1,0:T(8,128)(2,1)S(1)} %get-tuple-element.34), channel_id=1, source_target_pairs={{0,2},{2,0},{4,6},{6,4},{8,10},{10,8},{12,14},{14,12},{16,18},{18,... | collective-permute-start | bytes 368648 | tf_op jit(solution)/shard_map/ppermute | solution.py:125
  6.4 1.5 %collective-permute-start.27 = (bf16[480,128]{1,0:T(8,128)(2,1)S(1)}, bf16[480,128]{1,0:T(8,128)(2,1)S(1)}, u32[]{:S(2)}, u32[]{:S(2)}) collective-permute-start(bf16[480,128]{1,0:T(8,128)(2,1)S(1)} %get-tuple-element.35), channel_id=1, source_target_pairs={{0,4},{2,6},{4,0},{6,2},{8,12},{10,14},{12,8},{14,10},{16,20},{18,... | collective-permute-start | bytes 368648 | tf_op jit(solution)/shard_map/ppermute | solution.py:125
  8.0 2.0 %collective-permute-start.16 = (bf16[480,128]{1,0:T(8,128)(2,1)S(1)}, bf16[480,128]{1,0:T(8,128)(2,1)S(1)}, u32[]{:S(2)}, u32[]{:S(2)}) collective-permute-start(bf16[480,128]{1,0:T(8,128)(2,1)S(1)} %get-tuple-element.29), channel_id=1, source_target_pairs={{0,8},{2,10},{4,12},{6,14},{8,0},{10,2},{12,4},{14,6},{16,24},{18,... | collective-permute-start | bytes 368648 | tf_op jit(solution)/shard_map/ppermute | solution.py:125
  10.1 3.5 %collective-permute-start.18 = (bf16[480,128]{1,0:T(8,128)(2,1)S(1)}, bf16[480,128]{1,0:T(8,128)(2,1)S(1)}, u32[]{:S(2)}, u32[]{:S(2)}) collective-permute-start(bf16[480,128]{1,0:T(8,128)(2,1)S(1)} %get-tuple-element.30), channel_id=1, source_target_pairs={{0,10},{2,8},{4,14},{6,12},{8,2},{10,0},{12,6},{14,4},{16,26},{18,... | collective-permute-start | bytes 368648 | tf_op jit(solution)/shard_map/ppermute | solution.py:125
  13.9 2.4 %collective-permute-start.20 = (bf16[480,128]{1,0:T(8,128)(2,1)S(1)}, bf16[480,128]{1,0:T(8,128)(2,1)S(1)}, u32[]{:S(2)}, u32[]{:S(2)}) collective-permute-start(bf16[480,128]{1,0:T(8,128)(2,1)S(1)} %get-tuple-element.31), channel_id=1, source_target_pairs={{0,12},{2,14},{4,8},{6,10},{8,4},{10,6},{12,0},{14,2},{16,28},{18,... | collective-permute-start | bytes 368648 | tf_op jit(solution)/shard_map/ppermute | solution.py:125
  16.4 5.8 %collective-permute-start.12 = (bf16[480,128]{1,0:T(8,128)(2,1)S(1)}, bf16[480,128]{1,0:T(8,128)(2,1)S(1)}, u32[]{:S(2)}, u32[]{:S(2)}) collective-permute-start(bf16[480,128]{1,0:T(8,128)(2,1)S(1)} %get-tuple-element.27), channel_id=1, source_target_pairs={{0,30},{2,28},{4,26},{6,24},{8,22},{10,20},{12,18},{14,16},{16,14}... | collective-permute-start | bytes 368648 | tf_op jit(solution)/shard_map/ppermute | solution.py:125
  22.5 3.6 %collective-permute-start.10 = (bf16[480,128]{1,0:T(8,128)(2,1)S(1)}, bf16[480,128]{1,0:T(8,128)(2,1)S(1)}, u32[]{:S(2)}, u32[]{:S(2)}) collective-permute-start(bf16[480,128]{1,0:T(8,128)(2,1)S(1)} %get-tuple-element.26), channel_id=1, source_target_pairs={{0,24},{2,26},{4,28},{6,30},{8,16},{10,18},{12,20},{14,22},{16,8},... | collective-permute-start | bytes 368648 | tf_op jit(solution)/shard_map/ppermute | solution.py:125
  26.1 3.5 %collective-permute-start.4 = (bf16[480,128]{1,0:T(8,128)(2,1)S(1)}, bf16[480,128]{1,0:T(8,128)(2,1)S(1)}, u32[]{:S(2)}, u32[]{:S(2)}) collective-permute-start(bf16[480,128]{1,0:T(8,128)(2,1)S(1)} %get-tuple-element.23), channel_id=1, source_target_pairs={{0,22},{2,20},{4,18},{6,16},{8,30},{10,28},{12,26},{14,24},{16,6},... | collective-permute-start | bytes 368648 | tf_op jit(solution)/shard_map/ppermute | solution.py:125
  29.6 2.4 %collective-permute-done.12.refs_5_ = bf16[480,128]{1,0:T(8,128)(2,1)S(1)} collective-permute-done((bf16[480,128]{1,0:T(8,128)(2,1)S(1)}, bf16[480,128]{1,0:T(8,128)(2,1)S(1)}, u32[]{:S(2)}, u32[]{:S(2)}) %collective-permute-start.12) | collective-permute-done | bytes 122912 | tf_op jit(solution)/shard_map/ppermute | solution.py:125
  32.0 12.5 %collective-permute-start.6 = (bf16[480,128]{1,0:T(8,128)(2,1)S(1)}, bf16[480,128]{1,0:T(8,128)(2,1)S(1)}, u32[]{:S(2)}, u32[]{:S(2)}) collective-permute-start(bf16[480,128]{1,0:T(8,128)(2,1)S(1)} %get-tuple-element.24), channel_id=1, source_target_pairs={{0,20},{2,22},{4,16},{6,18},{8,28},{10,30},{12,24},{14,26},{16,4},... | collective-permute-start | bytes 368648 | tf_op jit(solution)/shard_map/ppermute | solution.py:125
  44.4 1.8 %collective-permute-start.2 = (bf16[480,128]{1,0:T(8,128)(2,1)S(1)}, bf16[480,128]{1,0:T(8,128)(2,1)S(1)}, u32[]{:S(2)}, u32[]{:S(2)}) collective-permute-start(bf16[480,128]{1,0:T(8,128)(2,1)S(1)} %get-tuple-element.22), channel_id=1, source_target_pairs={{0,18},{2,16},{4,22},{6,20},{8,26},{10,24},{12,30},{14,28},{16,2},... | collective-permute-start | bytes 368648 | tf_op jit(solution)/shard_map/ppermute | solution.py:125
  46.2 2.7 %collective-permute-start = (bf16[480,128]{1,0:T(8,128)(2,1)S(1)}, bf16[480,128]{1,0:T(8,128)(2,1)S(1)}, u32[]{:S(2)}, u32[]{:S(2)}) collective-permute-start(bf16[480,128]{1,0:T(8,128)(2,1)S(1)} %get-tuple-element.21), channel_id=1, source_target_pairs={{0,16},{2,18},{4,20},{6,22},{8,24},{10,26},{12,28},{14,30},{16,0},... | collective-permute-start | bytes 368648 | tf_op jit(solution)/shard_map/ppermute | solution.py:125
  48.9 8.7 %collective-permute-done.4.refs_5_ = bf16[480,128]{1,0:T(8,128)(2,1)S(1)} collective-permute-done((bf16[480,128]{1,0:T(8,128)(2,1)S(1)}, bf16[480,128]{1,0:T(8,128)(2,1)S(1)}, u32[]{:S(2)}, u32[]{:S(2)}) %collective-permute-start.4) | collective-permute-done | bytes 122912 | tf_op jit(solution)/shard_map/ppermute | solution.py:125
  57.6 2.1 %collective-permute-done.6.refs_7_ = bf16[480,128]{1,0:T(8,128)(2,1)S(1)} collective-permute-done((bf16[480,128]{1,0:T(8,128)(2,1)S(1)}, bf16[480,128]{1,0:T(8,128)(2,1)S(1)}, u32[]{:S(2)}, u32[]{:S(2)}) %collective-permute-start.6) | collective-permute-done | bytes 122912 | tf_op jit(solution)/shard_map/ppermute | solution.py:125
  59.7 2.8 %collective-permute-done.2.refs_5_ = bf16[480,128]{1,0:T(8,128)(2,1)S(1)} collective-permute-done((bf16[480,128]{1,0:T(8,128)(2,1)S(1)}, bf16[480,128]{1,0:T(8,128)(2,1)S(1)}, u32[]{:S(2)}, u32[]{:S(2)}) %collective-permute-start.2) | collective-permute-done | bytes 122912 | tf_op jit(solution)/shard_map/ppermute | solution.py:125
  65.4 1.4 %broadcast_select_fusion = (bf16[480,480]{1,0:T(8,128)(2,1)S(1)}, bf16[480,480]{1,0:T(8,128)(2,1)S(1)}) fusion(pred[]{:T(512)S(6)} %eq.23, bf16[480,960]{1,0:T(8,128)(2,1)} %fusion), kind=kLoop, calls=%fused_computation.2 | loop fusion | flops 460800 | bytes 1843201 | tf_op jit(solution)/shard_map/jit(_where)/select_n | solution.py:118
  68.5 3.9 %shard_map.73.refs_13_ = bf16[8,480,128]{2,1,0:T(8,128)(2,1)S(1)} custom-call(s32[32]{0:T(128)S(1)} %select_reduce_fusion.refs_0_, s32[1,15]{1,0:T(1,128)S(1)} %copy-done.1, f32[1,15]{1,0:T(1,128)S(1)} %copy-done.2, bf16[480,480]{1,0:T(8,128)(2,1)S(1)} %get-tuple-element.38.refs_3_, bf16[480,480]{1,0:T(8,128)(2,1)S(1)} %get-tuple-element.37.refs_4_, ...), custom_call_target="tpu_custom_call" | custom-call | flops 471859200 | bytes 3000000 | tf_op jit(solution)/shard_map/pallas_call | solution.py:140
  72.4 3.6 %shard_map.74.refs_9_ = bf16[8,480,128]{2,1,0:T(8,128)(2,1)S(1)} custom-call(s32[32]{0:T(128)S(1)} %select_reduce_fusion.refs_0_, s32[1,15]{1,0:T(1,128)S(1)} %copy-done.1, f32[1,15]{1,0:T(1,128)S(1)} %copy-done.2, bf16[480,480]{1,0:T(8,128)(2,1)S(1)} %get-tuple-element.38.refs_3_, ...), custom_call_target="tpu_custom_call", output_to_operand_aliasing={{}: (13, {})} | custom-call | flops 471859200 | bytes 3000000 | tf_op jit(solution)/shard_map/pallas_call | solution.py:140
  76.0 2.0 %shard_map.75.refs_9_ = bf16[8,480,128]{2,1,0:T(8,128)(2,1)S(1)} custom-call(s32[32]{0:T(128)S(1)} %select_reduce_fusion.refs_0_, s32[1,15]{1,0:T(1,128)S(1)} %copy-done.1, f32[1,15]{1,0:T(1,128)S(1)} %copy-done.2, bf16[480,480]{1,0:T(8,128)(2,1)S(1)} %get-tuple-element.38.refs_3_, ...), custom_call_target="tpu_custom_call", output_to_operand_aliasing={{}: (9, {})} | custom-call | flops 235929600 | bytes 3000000 | tf_op jit(solution)/shard_map/pallas_call | solution.py:140
  78.0 2.1 %shard_map.76.refs_9_ = bf16[8,480,128]{2,1,0:T(8,128)(2,1)S(1)} custom-call(s32[32]{0:T(128)S(1)} %select_reduce_fusion.refs_0_, s32[1,15]{1,0:T(1,128)S(1)} %copy-done.1, f32[1,15]{1,0:T(1,128)S(1)} %copy-done.2, bf16[480,480]{1,0:T(8,128)(2,1)S(1)} %get-tuple-element.38.refs_3_, ...), custom_call_target="tpu_custom_call", output_to_operand_aliasing={{}: (9, {})} | custom-call | flops 235929600 | bytes 3000000 | tf_op jit(solution)/shard_map/pallas_call | solution.py:140
  80.2 2.1 %shard_map.77.refs_7_ = bf16[8,480,128]{2,1,0:T(8,128)(2,1)S(1)} custom-call(s32[32]{0:T(128)S(1)} %select_reduce_fusion.refs_0_, s32[1,15]{1,0:T(1,128)S(1)} %copy-done.1, f32[1,15]{1,0:T(1,128)S(1)} %copy-done.2, bf16[480,480]{1,0:T(8,128)(2,1)S(1)} %get-tuple-element.38.refs_3_, ...), custom_call_target="tpu_custom_call", output_to_operand_aliasing={{}: (9, {})} | custom-call | flops 235929600 | bytes 3000000 | tf_op jit(solution)/shard_map/pallas_call | solution.py:140
  82.4 1.2 %shard_map.78.refs_7_ = bf16[8,480,128]{2,1,0:T(8,128)(2,1)S(1)} custom-call(s32[32]{0:T(128)S(1)} %select_reduce_fusion.refs_0_, s32[1,15]{1,0:T(1,128)S(1)} %copy-done.1, f32[1,15]{1,0:T(1,128)S(1)} %copy-done.2, bf16[480,480]{1,0:T(8,128)(2,1)S(1)} %get-tuple-element.38.refs_3_, ...), custom_call_target="tpu_custom_call", output_to_operand_aliasing={{}: (7, {})} | custom-call | flops 117964800 | bytes 3000000 | tf_op jit(solution)/shard_map/pallas_call | solution.py:140
  83.6 2.3 %shard_map.79 = bf16[1,480,960]{2,1,0:T(8,128)(2,1)} custom-call(s32[32]{0:T(128)S(1)} %select_reduce_fusion.refs_0_, s32[1,15]{1,0:T(1,128)S(1)} %copy-done.1, f32[1,15]{1,0:T(1,128)S(1)} %copy-done.2, bf16[480,480]{1,0:T(8,128)(2,1)S(1)} %get-tuple-element.38.refs_3_, bf16[480,480]{1,0:T(8,128)(2,1)S(1)} %get-tuple-element.37.refs_4_, ...), custom_call_target="tpu_custom_call" | custom-call | flops 117964800 | bytes 3000000 | tf_op jit(solution)/shard_map/pallas_call | solution.py:140
  (63 shorter events, 7.3 us)
Async XLA Ops:
  3.4 6.7 %collective-permute-start.25 = (bf16[480,128]{1,0:T(8,128)(2,1)S(1)}, bf16[480,128]{1,0:T(8,128)(2,1)S(1)}, u32[]{:S(2)}, u32[]{:S(2)}) collective-permute-start(bf16[480,128]{1,0:T(8,128)(2,1)S(1)} %get-tuple-element.34), channel_id=1, source_target_pairs={{0,2},{2,0},{4,6},{6,4},{8,10},{10,8},{12,14},{14,12},{16,18},{18,... | collective-permute-start | bytes 368648 | tf_op jit(solution)/shard_map/ppermute | solution.py:125
  6.4 7.5 %collective-permute-start.27 = (bf16[480,128]{1,0:T(8,128)(2,1)S(1)}, bf16[480,128]{1,0:T(8,128)(2,1)S(1)}, u32[]{:S(2)}, u32[]{:S(2)}) collective-permute-start(bf16[480,128]{1,0:T(8,128)(2,1)S(1)} %get-tuple-element.35), channel_id=1, source_target_pairs={{0,4},{2,6},{4,0},{6,2},{8,12},{10,14},{12,8},{14,10},{16,20},{18,... | collective-permute-start | bytes 368648 | tf_op jit(solution)/shard_map/ppermute | solution.py:125
  7.9 8.4 %collective-permute-start.29 = (bf16[480,128]{1,0:T(8,128)(2,1)S(1)}, bf16[480,128]{1,0:T(8,128)(2,1)S(1)}, u32[]{:S(2)}, u32[]{:S(2)}) collective-permute-start(bf16[480,128]{1,0:T(8,128)(2,1)S(1)} %get-tuple-element.36), channel_id=1, source_target_pairs={{0,6},{2,4},{4,2},{6,0},{8,14},{10,12},{12,10},{14,8},{16,22},{18,... | collective-permute-start | bytes 368648 | tf_op jit(solution)/shard_map/ppermute | solution.py:125
  8.0 8.4 %collective-permute-start.24 = (bf16[480,128]{1,0:T(8,128)(2,1)S(1)}, bf16[480,128]{1,0:T(8,128)(2,1)S(1)}, u32[]{:S(2)}, u32[]{:S(2)}) collective-permute-start(bf16[480,128]{1,0:T(8,128)(2,1)S(1)} %get-tuple-element.33.refs_5_), channel_id=1, source_target_pairs={{0,1},{1,0},{2,3},{3,2},{4,5},{5,4},{6,7},{7,6},{8,9},{9,8},{10,11... | collective-permute-start | bytes 368648 | tf_op jit(solution)/shard_map/ppermute | solution.py:127
  8.0 14.3 %collective-permute-start.16 = (bf16[480,128]{1,0:T(8,128)(2,1)S(1)}, bf16[480,128]{1,0:T(8,128)(2,1)S(1)}, u32[]{:S(2)}, u32[]{:S(2)}) collective-permute-start(bf16[480,128]{1,0:T(8,128)(2,1)S(1)} %get-tuple-element.29), channel_id=1, source_target_pairs={{0,8},{2,10},{4,12},{6,14},{8,0},{10,2},{12,4},{14,6},{16,24},{18,... | collective-permute-start | bytes 368648 | tf_op jit(solution)/shard_map/ppermute | solution.py:125
  10.1 12.4 %collective-permute-start.18 = (bf16[480,128]{1,0:T(8,128)(2,1)S(1)}, bf16[480,128]{1,0:T(8,128)(2,1)S(1)}, u32[]{:S(2)}, u32[]{:S(2)}) collective-permute-start(bf16[480,128]{1,0:T(8,128)(2,1)S(1)} %get-tuple-element.30), channel_id=1, source_target_pairs={{0,10},{2,8},{4,14},{6,12},{8,2},{10,0},{12,6},{14,4},{16,26},{18,... | collective-permute-start | bytes 368648 | tf_op jit(solution)/shard_map/ppermute | solution.py:125
  13.9 12.2 %collective-permute-start.20 = (bf16[480,128]{1,0:T(8,128)(2,1)S(1)}, bf16[480,128]{1,0:T(8,128)(2,1)S(1)}, u32[]{:S(2)}, u32[]{:S(2)}) collective-permute-start(bf16[480,128]{1,0:T(8,128)(2,1)S(1)} %get-tuple-element.31), channel_id=1, source_target_pairs={{0,12},{2,14},{4,8},{6,10},{8,4},{10,6},{12,0},{14,2},{16,28},{18,... | collective-permute-start | bytes 368648 | tf_op jit(solution)/shard_map/ppermute | solution.py:125
  16.4 9.8 %collective-permute-start.22 = (bf16[480,128]{1,0:T(8,128)(2,1)S(1)}, bf16[480,128]{1,0:T(8,128)(2,1)S(1)}, u32[]{:S(2)}, u32[]{:S(2)}) collective-permute-start(bf16[480,128]{1,0:T(8,128)(2,1)S(1)} %get-tuple-element.32), channel_id=1, source_target_pairs={{0,14},{2,12},{4,10},{6,8},{8,6},{10,4},{12,2},{14,0},{16,30},{18,... | collective-permute-start | bytes 368648 | tf_op jit(solution)/shard_map/ppermute | solution.py:125
  16.4 15.6 %collective-permute-start.12 = (bf16[480,128]{1,0:T(8,128)(2,1)S(1)}, bf16[480,128]{1,0:T(8,128)(2,1)S(1)}, u32[]{:S(2)}, u32[]{:S(2)}) collective-permute-start(bf16[480,128]{1,0:T(8,128)(2,1)S(1)} %get-tuple-element.27), channel_id=1, source_target_pairs={{0,30},{2,28},{4,26},{6,24},{8,22},{10,20},{12,18},{14,16},{16,14}... | collective-permute-start | bytes 368648 | tf_op jit(solution)/shard_map/ppermute | solution.py:125
  22.2 22.2 %collective-permute-start.14 = (bf16[480,128]{1,0:T(8,128)(2,1)S(1)}, bf16[480,128]{1,0:T(8,128)(2,1)S(1)}, u32[]{:S(2)}, u32[]{:S(2)}) collective-permute-start(bf16[480,128]{1,0:T(8,128)(2,1)S(1)} %get-tuple-element.28), channel_id=1, source_target_pairs={{0,28},{2,30},{4,24},{6,26},{8,20},{10,22},{12,16},{14,18},{16,12}... | collective-permute-start | bytes 368648 | tf_op jit(solution)/shard_map/ppermute | solution.py:125
  22.5 23.7 %collective-permute-start.10 = (bf16[480,128]{1,0:T(8,128)(2,1)S(1)}, bf16[480,128]{1,0:T(8,128)(2,1)S(1)}, u32[]{:S(2)}, u32[]{:S(2)}) collective-permute-start(bf16[480,128]{1,0:T(8,128)(2,1)S(1)} %get-tuple-element.26), channel_id=1, source_target_pairs={{0,24},{2,26},{4,28},{6,30},{8,16},{10,18},{12,20},{14,22},{16,8},... | collective-permute-start | bytes 368648 | tf_op jit(solution)/shard_map/ppermute | solution.py:125
  26.1 22.8 %collective-permute-start.8 = (bf16[480,128]{1,0:T(8,128)(2,1)S(1)}, bf16[480,128]{1,0:T(8,128)(2,1)S(1)}, u32[]{:S(2)}, u32[]{:S(2)}) collective-permute-start(bf16[480,128]{1,0:T(8,128)(2,1)S(1)} %get-tuple-element.25), channel_id=1, source_target_pairs={{0,26},{2,24},{4,30},{6,28},{8,18},{10,16},{12,22},{14,20},{16,10}... | collective-permute-start | bytes 368648 | tf_op jit(solution)/shard_map/ppermute | solution.py:125
  26.1 31.5 %collective-permute-start.4 = (bf16[480,128]{1,0:T(8,128)(2,1)S(1)}, bf16[480,128]{1,0:T(8,128)(2,1)S(1)}, u32[]{:S(2)}, u32[]{:S(2)}) collective-permute-start(bf16[480,128]{1,0:T(8,128)(2,1)S(1)} %get-tuple-element.23), channel_id=1, source_target_pairs={{0,22},{2,20},{4,18},{6,16},{8,30},{10,28},{12,26},{14,24},{16,6},... | collective-permute-start | bytes 368648 | tf_op jit(solution)/shard_map/ppermute | solution.py:125
  32.0 27.8 %collective-permute-start.6 = (bf16[480,128]{1,0:T(8,128)(2,1)S(1)}, bf16[480,128]{1,0:T(8,128)(2,1)S(1)}, u32[]{:S(2)}, u32[]{:S(2)}) collective-permute-start(bf16[480,128]{1,0:T(8,128)(2,1)S(1)} %get-tuple-element.24), channel_id=1, source_target_pairs={{0,20},{2,22},{4,16},{6,18},{8,28},{10,30},{12,24},{14,26},{16,4},... | collective-permute-start | bytes 368648 | tf_op jit(solution)/shard_map/ppermute | solution.py:125
  44.4 18.1 %collective-permute-start.2 = (bf16[480,128]{1,0:T(8,128)(2,1)S(1)}, bf16[480,128]{1,0:T(8,128)(2,1)S(1)}, u32[]{:S(2)}, u32[]{:S(2)}) collective-permute-start(bf16[480,128]{1,0:T(8,128)(2,1)S(1)} %get-tuple-element.22), channel_id=1, source_target_pairs={{0,18},{2,16},{4,22},{6,20},{8,26},{10,24},{12,30},{14,28},{16,2},... | collective-permute-start | bytes 368648 | tf_op jit(solution)/shard_map/ppermute | solution.py:125
  46.2 16.3 %collective-permute-start = (bf16[480,128]{1,0:T(8,128)(2,1)S(1)}, bf16[480,128]{1,0:T(8,128)(2,1)S(1)}, u32[]{:S(2)}, u32[]{:S(2)}) collective-permute-start(bf16[480,128]{1,0:T(8,128)(2,1)S(1)} %get-tuple-element.21), channel_id=1, source_target_pairs={{0,16},{2,18},{4,20},{6,22},{8,24},{10,26},{12,28},{14,30},{16,0},... | collective-permute-start | bytes 368648 | tf_op jit(solution)/shard_map/ppermute | solution.py:125
  48.9 15.3 %collective-permute-start.26 = (bf16[480,128]{1,0:T(8,128)(2,1)S(1)}, bf16[480,128]{1,0:T(8,128)(2,1)S(1)}, u32[]{:S(2)}, u32[]{:S(2)}) collective-permute-start(bf16[480,128]{1,0:T(8,128)(2,1)S(1)} %collective-permute-done.25.refs_7_), channel_id=1, source_target_pairs={{0,1},{1,0},{2,3},{3,2},{4,5},{5,4},{6,7},{7,6},{8,9},{9,8},{10,11... | collective-permute-start | bytes 368648 | tf_op jit(solution)/shard_map/ppermute | solution.py:127
  57.6 6.7 %collective-permute-start.28 = (bf16[480,128]{1,0:T(8,128)(2,1)S(1)}, bf16[480,128]{1,0:T(8,128)(2,1)S(1)}, u32[]{:S(2)}, u32[]{:S(2)}) collective-permute-start(bf16[480,128]{1,0:T(8,128)(2,1)S(1)} %collective-permute-done.27.refs_9_), channel_id=1, source_target_pairs={{0,1},{1,0},{2,3},{3,2},{4,5},{5,4},{6,7},{7,6},{8,9},{9,8},{10,11... | collective-permute-start | bytes 368648 | tf_op jit(solution)/shard_map/ppermute | solution.py:127
  59.7 5.1 %collective-permute-start.30 = (bf16[480,128]{1,0:T(8,128)(2,1)S(1)}, bf16[480,128]{1,0:T(8,128)(2,1)S(1)}, u32[]{:S(2)}, u32[]{:S(2)}) collective-permute-start(bf16[480,128]{1,0:T(8,128)(2,1)S(1)} %collective-permute-done.29.refs_11_), channel_id=1, source_target_pairs={{0,1},{1,0},{2,3},{3,2},{4,5},{5,4},{6,7},{7,6},{8,9},{9,8},{10,11... | collective-permute-start | bytes 368648 | tf_op jit(solution)/shard_map/ppermute | solution.py:127
  66.9 11.2 %collective-permute-start.9 = (bf16[480,128]{1,0:T(8,128)(2,1)S(1)}, bf16[480,128]{1,0:T(8,128)(2,1)S(1)}, u32[]{:S(2)}, u32[]{:S(2)}) collective-permute-start(bf16[480,128]{1,0:T(8,128)(2,1)S(1)} %collective-permute-done.8.refs_5_), channel_id=1, source_target_pairs={{0,1},{1,0},{2,3},{3,2},{4,5},{5,4},{6,7},{7,6},{8,9},{9,8},{10,11... | collective-permute-start | bytes 368648 | tf_op jit(solution)/shard_map/ppermute | solution.py:127
  67.4 12.7 %collective-permute-start.5 = (bf16[480,128]{1,0:T(8,128)(2,1)S(1)}, bf16[480,128]{1,0:T(8,128)(2,1)S(1)}, u32[]{:S(2)}, u32[]{:S(2)}) collective-permute-start(bf16[480,128]{1,0:T(8,128)(2,1)S(1)} %collective-permute-done.4.refs_5_), channel_id=1, source_target_pairs={{0,1},{1,0},{2,3},{3,2},{4,5},{5,4},{6,7},{7,6},{8,9},{9,8},{10,11... | collective-permute-start | bytes 368648 | tf_op jit(solution)/shard_map/ppermute | solution.py:127
  67.6 12.6 %collective-permute-start.7 = (bf16[480,128]{1,0:T(8,128)(2,1)S(1)}, bf16[480,128]{1,0:T(8,128)(2,1)S(1)}, u32[]{:S(2)}, u32[]{:S(2)}) collective-permute-start(bf16[480,128]{1,0:T(8,128)(2,1)S(1)} %collective-permute-done.6.refs_7_), channel_id=1, source_target_pairs={{0,1},{1,0},{2,3},{3,2},{4,5},{5,4},{6,7},{7,6},{8,9},{9,8},{10,11... | collective-permute-start | bytes 368648 | tf_op jit(solution)/shard_map/ppermute | solution.py:127
  68.0 14.3 %collective-permute-start.3 = (bf16[480,128]{1,0:T(8,128)(2,1)S(1)}, bf16[480,128]{1,0:T(8,128)(2,1)S(1)}, u32[]{:S(2)}, u32[]{:S(2)}) collective-permute-start(bf16[480,128]{1,0:T(8,128)(2,1)S(1)} %collective-permute-done.2.refs_5_), channel_id=1, source_target_pairs={{0,1},{1,0},{2,3},{3,2},{4,5},{5,4},{6,7},{7,6},{8,9},{9,8},{10,11... | collective-permute-start | bytes 368648 | tf_op jit(solution)/shard_map/ppermute | solution.py:127
  68.1 15.5 %collective-permute-start.1 = (bf16[480,128]{1,0:T(8,128)(2,1)S(1)}, bf16[480,128]{1,0:T(8,128)(2,1)S(1)}, u32[]{:S(2)}, u32[]{:S(2)}) collective-permute-start(bf16[480,128]{1,0:T(8,128)(2,1)S(1)} %collective-permute-done.refs_5_), channel_id=1, source_target_pairs={{0,1},{1,0},{2,3},{3,2},{4,5},{5,4},{6,7},{7,6},{8,9},{9,8},{10,11... | collective-permute-start | bytes 368648 | tf_op jit(solution)/shard_map/ppermute | solution.py:127
  (14 other events, 155.6 us)
